TPU v7x, 32 devices: a whole 2x2x4 slice. The times are simulated.
32 devices in a mesh: rows: 8 (over z, x), cols: 4 (over y, core).
Axes of the slice: x: 2, y: 2, z: 4, core: 2. Of those that a mesh axis runs over, the one named last changes fastest.
Arguments:
- basis: float32 [8192, 4096], P('rows', 'cols'), may hold values from -119.66257 to 119.66257, as said below
- block: float32 [8192, 512], P('rows', 'cols'), may hold values from -1800 to 1800
Outputs:
- ortho: float32 [8192, 512], P('rows', 'cols')
- factors: float32 [4, 128, 128], P('cols')
Inputs may be any that keep to these rules, and one draw needn't show every extreme that they name: Under the inner product (sum over rows divided by 8192) the basis columns have squared norms between 0.6 and 1.9, and inner products of distinct basis columns are at most 0.05 in magnitude.
All inputs are finite; a program needn't handle non-finite values.
Results may differ from a plain program's by a relative error of at most 0.000076.
Values sent between devices are 32-bit elements; how exact they have to be, the bound alone decides.
No kernel may reach another device: no remote copies, remote signals or barrier semaphores. Data moves between devices by JAX's collectives and lax.ppermute only.
A program may use at most 64 MiB of HBM per device.

v0:
```python
import jax
import jax.numpy as jnp
from jax import lax
from jax.sharding import PartitionSpec as P

BLK = 128


def solve_block(lower_factor, vectors):
    return jax.scipy.linalg.solve_triangular(lower_factor, vectors, lower=True)


def body(basis, block):
    highest = lax.Precision.HIGHEST
    local_rows = basis.shape[0]
    inverse = 1.0 / (local_rows * lax.axis_size("rows"))
    width = block.shape[1]
    column_index = lax.axis_index("cols")

    def project(piece):
        return (
            lax.dot_general(
                basis,
                piece,
                (((0,), (0,)), ((), ())),
                precision=highest,
                preferred_element_type=jnp.float32,
            )
            * inverse
        )

    def expand(coef):
        return jnp.dot(basis, coef, precision=highest, preferred_element_type=jnp.float32)

    terms_one = project(lax.all_gather(block, "cols", axis=1, tiled=True))
    coef_one = lax.psum(terms_one, "rows")
    placed = lax.dynamic_update_slice_in_dim(
        jnp.zeros((local_rows, coef_one.shape[1]), jnp.float32), block, column_index * width, 1
    )
    first_whole = lax.psum(placed - expand(coef_one), "cols")
    terms_two = project(first_whole)
    first = lax.dynamic_slice_in_dim(first_whole, column_index * width, width, 1)
    coef_two = lax.psum(terms_two, "rows")
    second = first - lax.psum_scatter(expand(coef_two), "cols", scatter_dimension=1, tiled=True)
    blocks = width // BLK
    pieces = second.reshape(local_rows, blocks, BLK)
    gram = jnp.einsum("mbi,mbj->bij", pieces, pieces, precision=highest) * inverse
    gram = lax.psum(gram, "rows")
    lower_factor = jnp.linalg.cholesky(gram)
    solved = jax.vmap(solve_block)(lower_factor, jnp.transpose(pieces, (1, 2, 0)))
    ortho = jnp.transpose(solved, (2, 0, 1)).reshape(local_rows, width)
    return (ortho, jnp.transpose(lower_factor, (0, 2, 1)))


def solution(mesh):
    placed = (P("rows", "cols"), P("rows", "cols"))
    return jax.shard_map(
        body,
        mesh=mesh,
        in_specs=placed,
        out_specs=(P("rows", "cols"), P("cols", None, None)),
        check_vma=False,
    )
```

profile of v0, /device:TPU:0, one launch (start us, length us, event | category | flops | bytes accessed | tf_op | source)
XLA Modules:
  0.0 476.0 jit_solution(7517272405939530119)
XLA Ops:
  7.2 0.0 all-gather.2.cloned.1.call-start
  7.2 0.7 all-gather.2.cloned.1.call-update
  7.9 0.0 all-reduce.5.cloned.1.call-start
  7.9 27.2 %all-gather.2.cloned.1.call-done = f32[1024,512]{1,0:T(8,128)} async-done(((f32[1024,128]{1,0:T(8,128)}), f32[1024,512]{1,0:T(8,128)}) %all-gather.2.cloned.1.call-update) | async-done | bytes 2097168 | tf_op jit(solution)/shard_map/all_gather | solution.py:35
  35.1 10.2 %convolution_multiply_fusion = f32[1024,512]{1,0:T(8,128)} fusion(f32[1024,1024]{1,0:T(8,128)} %param.2, f32[1024,512]{1,0:T(8,128)} %all-gather.2.cloned.1.call-done), kind=kOutput, calls=%fused_computation.3 | convolution fusion | flops 6442975232 | bytes 8388608 | tf_op jit(solution)/shard_map/dot_general | solution.py:22
  45.3 0.0 copy-start.1
  45.3 0.0 all-reduce.5.cloned.1.call-update
  45.3 0.0 all-reduce.7.cloned.1.call-start
  45.4 1.0 copy-done.1
  46.3 0.2 copy.4
  46.5 0.2 broadcast_in_dim.7
  46.8 0.1 constant_dynamic-update-slice_fusion
  46.8 100.9 %all-reduce.5.cloned.1.call-done = f32[1024,512]{1,0:T(8,128)} async-done(((f32[1024,512]{1,0:T(8,128)}), f32[1024,512]{1,0:T(8,128)}) %all-reduce.5.cloned.1.call-update) | async-done | bytes 2097168 | tf_op jit(solution)/shard_map/psum | solution.py:36
  147.8 16.7 %bitcast_subtract_fusion = f32[1024,512]{0,1:T(8,128)} fusion(f32[1024,512]{0,1:T(8,128)S(1)} %constant_dynamic-update-slice_fusion, f32[1024,512]{1,0:T(8,128)} %all-reduce.5.cloned.1.call-done, f32[1024,1024]{1,0:T(8,128)} %param.2), kind=kOutput, calls=%fused_computation | convolution fusion | flops 6442975232 | bytes 10485760 | tf_op jit(solution)/shard_map/dot_general | solution.py:33
  164.5 0.0 all-reduce.7.cloned.1.call-update
  164.5 0.2 all-reduce.9.cloned.1.call-start
  164.7 50.6 %all-reduce.7.cloned.1.call-done = f32[1024,512]{0,1:T(8,128)} async-done(((f32[1024,512]{0,1:T(8,128)}), f32[1024,512]{0,1:T(8,128)}) %all-reduce.7.cloned.1.call-update) | async-done | bytes 2097168 | tf_op jit(solution)/shard_map/psum | solution.py:40
  215.3 10.2 %multiply_bitcast_fusion = f32[1024,512]{0,1:T(8,128)} fusion(f32[1024,512]{0,1:T(8,128)} %all-reduce.7.cloned.1.call-done, f32[1024,1024]{1,0:T(8,128)} %param.2), kind=kOutput, calls=%fused_computation.1 | convolution fusion | flops 6442975232 | bytes 8388608 | tf_op jit(solution)/shard_map/dot_general | solution.py:22
  225.6 0.0 all-reduce.9.cloned.1.call-update
  225.6 0.0 reduce-scatter.2.cloned.1.call-start
  225.6 102.5 %all-reduce.9.cloned.1.call-done = f32[1024,512]{0,1:T(8,128)} async-done(((f32[1024,512]{0,1:T(8,128)}), f32[1024,512]{0,1:T(8,128)}) %all-reduce.9.cloned.1.call-update) | async-done | bytes 2097168 | tf_op jit(solution)/shard_map/psum | solution.py:43
  328.1 10.3 %convolution_bitcast_fusion = f32[1024,512]{0,1:T(8,128)} fusion(f32[1024,512]{0,1:T(8,128)} %all-reduce.9.cloned.1.call-done, f32[1024,1024]{1,0:T(8,128)} %param.2), kind=kOutput, calls=%fused_computation.2 | convolution fusion | flops 6442450944 | bytes 8388608 | tf_op jit(solution)/shard_map/dot_general | solution.py:33
  338.4 0.0 copy-start
  338.4 0.0 reduce-scatter.2.cloned.1.call-update
  338.4 0.3 all-reduce.11.cloned.1.call-start
  338.7 30.3 %reduce-scatter.2.cloned.1.call-done = f32[1024,128]{0,1:T(8,128)} async-done(((f32[1024,512]{0,1:T(8,128)}), f32[1024,128]{0,1:T(8,128)}) %reduce-scatter.2.cloned.1.call-update) | async-done | bytes 524304 | tf_op jit(solution)/shard_map/reduce_scatter | solution.py:44
  369.0 0.0 copy-done
  369.0 0.0 copy-start.2
  369.0 2.5 fusion
  371.5 0.0 all-reduce.11.cloned.1.call-update
  371.5 70.6 %all-reduce.11.cloned.1.call-done = f32[1,128,128]{1,2,0:T(8,128)} async-done(((f32[1,128,128]{1,2,0:T(8,128)}), f32[1,128,128]{1,2,0:T(8,128)}) %all-reduce.11.cloned.1.call-update) | async-done | bytes 65552 | tf_op jit(solution)/shard_map/psum | solution.py:48
  442.2 0.9 copy.6
  443.1 0.9 fusion.3
  444.0 11.7 %custom-call.8 = f32[1,128,128]{2,1,0:T(8,128)S(1)} custom-call(f32[1,128,128]{2,1,0:T(8,128)S(1)} %fusion.3), custom_call_target="Cholesky" | custom-call | tf_op jit(solution)/shard_map/jit(cholesky)/cholesky | solution.py:49
  455.7 0.6 compare_reduce_fusion
  456.4 0.7 fusion.4
  457.0 9.8 %custom-call.9 = f32[1,1,128,128]{2,3,1,0:T(8,128)S(1)} custom-call(f32[1,1,128,128]{3,2,1,0:T(8,128)S(1)} %get-tuple-element.5), custom_call_target="InvertDiagBlocksLowerTriangular" | custom-call | tf_op jit(solution)/shard_map/vmap(jit(_solve_triangular))/triangular_solve | solution.py:10
  466.8 0.0 copy-done.2
  466.8 0.6 convolution_bitcast_fusion.1
  467.5 1.0 copy.7
  468.5 0.7 copy.8
  (1 shorter events, 0.0 us)
Async XLA Ops:
  7.2 27.9 %all-gather.2.cloned.1.call-start = ((), (), s32[]{:S(2)}) async-start(), calls=%async_computation.1 | async-start | bytes 2621440 | tf_op jit(solution)/shard_map/all_gather | solution.py:35
  7.9 139.9 %all-reduce.5.cloned.1.call-start = ((), (), s32[]{:S(2)}) async-start(), calls=%async_computation.2 | async-start | bytes 4194304 | tf_op jit(solution)/shard_map/psum | solution.py:36
  45.3 1.0 copy-start.1
  45.3 170.0 %all-reduce.7.cloned.1.call-start = ((), (), s32[]{:S(2)}) async-start(), calls=%async_computation.3 | async-start | bytes 4194304 | tf_op jit(solution)/shard_map/psum | solution.py:40
  164.5 163.6 %all-reduce.9.cloned.1.call-start = ((), (), s32[]{:S(2)}) async-start(), calls=%async_computation.4 | async-start | bytes 4194304 | tf_op jit(solution)/shard_map/psum | solution.py:43
  225.6 143.4 %reduce-scatter.2.cloned.1.call-start = ((), (), s32[]{:S(2)}) async-start(), calls=%async_computation.5 | async-start | bytes 2621440 | tf_op jit(solution)/shard_map/reduce_scatter | solution.py:44
  338.4 30.6 %copy-start = (f32[1024,512]{0,1:T(8,128)S(1)}, f32[1024,512]{0,1:T(8,128)}, u32[]{:S(2)}) copy-start(f32[1024,512]{0,1:T(8,128)} %all-reduce.7.cloned.1.call-done) | copy-start | bytes 6291460
  338.4 103.8 %all-reduce.11.cloned.1.call-start = ((), (), s32[]{:S(2)}) async-start(), calls=%async_computation.6 | async-start | bytes 131072 | tf_op jit(solution)/shard_map/psum | solution.py:48
  369.0 97.8 %copy-start.2 = (f32[1024,128]{0,1:T(8,128)S(1)}, f32[1024,128]{0,1:T(8,128)}, u32[]{:S(2)}) copy-start(f32[1024,128]{0,1:T(8,128)} %reduce-scatter.2.cloned.1.call-done) | copy-start | bytes 1572868
Sparse Core Ops, SparseCore 0:
  9.5 25.5 all-gather.1
  45.4 102.3 all-reduce.4
  164.6 50.6 all-reduce.6
  225.7 102.3 all-reduce.8
  338.5 30.4 reduce-scatter.1
  372.9 69.2 all-reduce.10
where the time goes:
time: 476 us
  waiting for transfers between devices  383 us (80%)
  matrix products  50.5 us (11%)
  other arithmetic  23.7 us (5%)
  between operations  14.2 us (3%)
    psum x1, waiting for transfers between devices, body(): coef_two = lax.psum(terms_two, 'rows')  102 us
    psum x1, waiting for transfers between devices, body(): coef_one = lax.psum(terms_one, 'rows')  101 us
    psum x1, waiting for transfers between devices, body(): gram = lax.psum(gram, 'rows')  70.6 us
    psum x1, waiting for transfers between devices, body(): first_whole = lax.psum(placed - expand(coef_one), 'cols')  50.6 us
    reduce_scatter x1, waiting for transfers between devices, body(): lax.psum_scatter(expand(coef_two), 'cols', scatter_dimension=1, tiled=True)  30.3 us
    all_gather x1, waiting for transfers between devices, body(): terms_one = project(lax.all_gather(block, 'cols', axis=1, tiled=True))  27.2 us
    dot_general x2, matrix products, expand(): jnp.dot(basis, coef, precision=highest, preferred_element_type=jnp.float32)  27 us
    dot_general x2, matrix products, project(): lax.dot_general(basis, piece, (((0,), (0,)), ((), ())), precision=highest...  20.4 us
  transfers between devices with their start and end apart: 6, of which 6 were waited for; matrix products, arithmetic and copies ran while one was open for 0% of the time, Pallas kernels for 0%

commit v1 on v0

--- a/solution.py
+++ b/solution.py
@@ -37,7 +37,7 @@
     placed = lax.dynamic_update_slice_in_dim(
         jnp.zeros((local_rows, coef_one.shape[1]), jnp.float32), block, column_index * width, 1
     )
-    first_whole = lax.psum(placed - expand(coef_one), "cols")
+    first_whole = jnp.sum(lax.all_gather(placed - expand(coef_one), "cols"), axis=0)
     terms_two = project(first_whole)
     first = lax.dynamic_slice_in_dim(first_whole, column_index * width, width, 1)
     coef_two = lax.psum(terms_two, "rows")

time: 476 us -> 502 us (1.055)
  local copies, waits for them, and re-layouts: 4.11 us -> 14.9 us
  other arithmetic: 23.7 us -> 32.2 us
  waiting for transfers between devices: 383 us -> 390 us
    all_gather x0 -> x1, waiting for transfers between devices: none -> 57.5 us  [body(): lax.all_gather(placed - expand(coef_one), 'cols')]
    psum x1 -> x0, waiting for transfers between devices: 50.6 us -> none  [body(): first_whole = lax.psum(placed - expand(coef_one), 'cols')]
    all_gather x0 -> x1, local copies, waits for them, and re-layouts: none -> 10.8 us  [body(): lax.all_gather(placed - expand(coef_one), 'cols')]
    reduce_sum x0 -> x1, other arithmetic: none -> 8.49 us  [body(): jnp.sum(lax.all_gather(placed - expand(coef_one), 'cols'), axis=0)]
where the time goes in v1:
time: 502 us
  waiting for transfers between devices  390 us (78%)
  matrix products  49.9 us (10%)
  other arithmetic  32.2 us (6%)
  local copies, waits for them, and re-layouts  14.9 us (3%)
  between operations  14.2 us (3%)
    psum x1, waiting for transfers between devices, body(): coef_two = lax.psum(terms_two, 'rows')  102 us
    psum x1, waiting for transfers between devices, body(): coef_one = lax.psum(terms_one, 'rows')  101 us
    psum x1, waiting for transfers between devices, body(): gram = lax.psum(gram, 'rows')  70.6 us
    all_gather x1, waiting for transfers between devices, body(): lax.all_gather(placed - expand(coef_one), 'cols')  57.5 us
    reduce_scatter x1, waiting for transfers between devices, body(): lax.psum_scatter(expand(coef_two), 'cols', scatter_dimension=1, tiled=True)  30.6 us
    all_gather x1, waiting for transfers between devices, body(): terms_one = project(lax.all_gather(block, 'cols', axis=1, tiled=True))  27.2 us
    dot_general x2, matrix products, expand(): jnp.dot(basis, coef, precision=highest, preferred_element_type=jnp.float32)  27 us
    dot_general x2, matrix products, project(): lax.dot_general(basis, piece, (((0,), (0,)), ((), ())), precision=highest...  19.8 us
  transfers between devices with their start and end apart: 6, of which 6 were waited for; matrix products, arithmetic and copies ran while one was open for 0% of the time, Pallas kernels for 0%

profile of v1, /device:TPU:0, one launch (start us, length us, event | category | flops | bytes accessed | tf_op | source)
XLA Modules:
  0.0 501.5 jit_solution(5086193454067057085)
XLA Ops:
  7.2 0.0 all-gather.4.cloned.1.call-start
  7.2 0.7 all-gather.4.cloned.1.call-update
  7.9 0.0 all-reduce.4.cloned.1.call-start
  7.9 27.2 %all-gather.4.cloned.1.call-done = f32[1024,512]{1,0:T(8,128)} async-done(((f32[1024,128]{1,0:T(8,128)}), f32[1024,512]{1,0:T(8,128)}) %all-gather.4.cloned.1.call-update) | async-done | bytes 2097168 | tf_op jit(solution)/shard_map/all_gather | solution.py:35
  35.1 10.2 %convolution_multiply_fusion = f32[1024,512]{1,0:T(8,128)} fusion(f32[1024,1024]{1,0:T(8,128)} %param.2, f32[1024,512]{1,0:T(8,128)} %all-gather.4.cloned.1.call-done), kind=kOutput, calls=%fused_computation.3 | convolution fusion | flops 6442975232 | bytes 8388608 | tf_op jit(solution)/shard_map/dot_general | solution.py:22
  45.3 0.0 copy-start
  45.3 0.0 all-reduce.4.cloned.1.call-update
  45.3 0.0 all-gather.6.cloned.1.call-start
  45.4 1.0 copy-done
  46.3 0.2 copy.4
  46.5 0.2 broadcast_in_dim.7
  46.8 0.1 constant_dynamic-update-slice_fusion
  46.9 100.9 %all-reduce.4.cloned.1.call-done = f32[1024,512]{1,0:T(8,128)} async-done(((f32[1024,512]{1,0:T(8,128)}), f32[1024,512]{1,0:T(8,128)}) %all-reduce.4.cloned.1.call-update) | async-done | bytes 2097168 | tf_op jit(solution)/shard_map/psum | solution.py:36
  147.8 16.7 %bitcast_subtract_fusion = f32[1024,512]{0,1:T(8,128)} fusion(f32[1024,512]{0,1:T(8,128)S(1)} %constant_dynamic-update-slice_fusion, f32[1024,512]{1,0:T(8,128)} %all-reduce.4.cloned.1.call-done, f32[1024,1024]{1,0:T(8,128)} %param.2), kind=kOutput, calls=%fused_computation | convolution fusion | flops 6442975232 | bytes 10485760 | tf_op jit(solution)/shard_map/dot_general | solution.py:33
  164.5 0.0 all-gather.6.cloned.1.call-update
  164.5 0.2 all-reduce.6.cloned.1.call-start
  164.7 57.5 %all-gather.6.cloned.1.call-done = f32[4096,512]{0,1:T(8,128)} async-done(((f32[1024,512]{0,1:T(8,128)}), f32[4096,512]{0,1:T(8,128)}) %all-gather.6.cloned.1.call-update) | async-done | bytes 8388624 | tf_op jit(solution)/shard_map/all_gather | solution.py:40
  222.2 10.8 %reshape.74 = f32[4,1024,512]{1,0,2:T(4,128)} reshape(f32[4096,512]{0,1:T(8,128)} %all-gather.6.cloned.1.call-done) | data formatting | bytes 16777216 | tf_op jit(solution)/shard_map/all_gather | solution.py:40
  233.0 8.5 %reduce_sum.9 = f32[1024,512]{0,1:T(8,128)S(1)} reduce(f32[4,1024,512]{1,0,2:T(4,128)} %reshape.74, f32[]{:T(128)} %constant.52.clone.1), dimensions={0}, to_apply=%region_1.0 | reduce | flops 1572864 | bytes 10485764 | tf_op jit(solution)/shard_map/reduce_sum | solution.py:40
  241.5 9.6 %multiply_bitcast_fusion = f32[1024,512]{0,1:T(8,128)} fusion(f32[1024,512]{0,1:T(8,128)S(1)} %reduce_sum.9, f32[1024,1024]{1,0:T(8,128)} %param.2), kind=kOutput, calls=%fused_computation.1 | convolution fusion | flops 6442975232 | bytes 8388608 | tf_op jit(solution)/shard_map/dot_general | solution.py:22
  251.2 0.0 all-reduce.6.cloned.1.call-update
  251.2 0.3 reduce-scatter.2.cloned.1.call-start
  251.4 102.2 %all-reduce.6.cloned.1.call-done = f32[1024,512]{0,1:T(8,128)} async-done(((f32[1024,512]{0,1:T(8,128)}), f32[1024,512]{0,1:T(8,128)}) %all-reduce.6.cloned.1.call-update) | async-done | bytes 2097168 | tf_op jit(solution)/shard_map/psum | solution.py:43
  353.6 10.3 %convolution_bitcast_fusion = f32[1024,512]{0,1:T(8,128)} fusion(f32[1024,512]{0,1:T(8,128)} %all-reduce.6.cloned.1.call-done, f32[1024,1024]{1,0:T(8,128)} %param.2), kind=kOutput, calls=%fused_computation.2 | convolution fusion | flops 6442450944 | bytes 8388608 | tf_op jit(solution)/shard_map/dot_general | solution.py:33
  363.9 0.0 reduce-scatter.2.cloned.1.call-update
  363.9 0.0 all-reduce.8.cloned.1.call-start
  364.0 30.6 %reduce-scatter.2.cloned.1.call-done = f32[1024,128]{0,1:T(8,128)} async-done(((f32[1024,512]{0,1:T(8,128)}), f32[1024,128]{0,1:T(8,128)}) %reduce-scatter.2.cloned.1.call-update) | async-done | bytes 524304 | tf_op jit(solution)/shard_map/reduce_scatter | solution.py:44
  394.5 0.0 copy-start.1
  394.5 2.5 fusion
  397.0 0.0 all-reduce.8.cloned.1.call-update
  397.1 70.6 %all-reduce.8.cloned.1.call-done = f32[1,128,128]{1,2,0:T(8,128)} async-done(((f32[1,128,128]{1,2,0:T(8,128)}), f32[1,128,128]{1,2,0:T(8,128)}) %all-reduce.8.cloned.1.call-update) | async-done | bytes 65552 | tf_op jit(solution)/shard_map/psum | solution.py:48
  467.7 0.9 copy.6
  468.6 0.9 fusion.3
  469.5 11.7 %custom-call.8 = f32[1,128,128]{2,1,0:T(8,128)S(1)} custom-call(f32[1,128,128]{2,1,0:T(8,128)S(1)} %fusion.3), custom_call_target="Cholesky" | custom-call | tf_op jit(solution)/shard_map/jit(cholesky)/cholesky | solution.py:49
  481.2 0.6 compare_reduce_fusion
  481.8 0.7 fusion.4
  482.5 0.7 copy.8
  483.2 9.8 %custom-call.9 = f32[1,1,128,128]{2,3,1,0:T(8,128)S(1)} custom-call(f32[1,1,128,128]{3,2,1,0:T(8,128)S(1)} %get-tuple-element.5), custom_call_target="InvertDiagBlocksLowerTriangular" | custom-call | tf_op jit(solution)/shard_map/vmap(jit(_solve_triangular))/triangular_solve | solution.py:10
  493.1 0.0 copy-done.1
  493.1 0.6 convolution_bitcast_fusion.1
  493.7 1.0 copy.7
  (1 shorter events, 0.0 us)
Async XLA Ops:
  7.2 27.9 %all-gather.4.cloned.1.call-start = ((), (), s32[]{:S(2)}) async-start(), calls=%async_computation.1 | async-start | bytes 2621440 | tf_op jit(solution)/shard_map/all_gather | solution.py:35
  7.9 139.9 %all-reduce.4.cloned.1.call-start = ((), (), s32[]{:S(2)}) async-start(), calls=%async_computation.2 | async-start | bytes 4194304 | tf_op jit(solution)/shard_map/psum | solution.py:36
  45.3 1.0 copy-start
  45.3 176.9 %all-gather.6.cloned.1.call-start = ((), (), s32[]{:S(2)}) async-start(), calls=%async_computation.6 | async-start | bytes 10485760 | tf_op jit(solution)/shard_map/all_gather | solution.py:40
  164.5 189.1 %all-reduce.6.cloned.1.call-start = ((), (), s32[]{:S(2)}) async-start(), calls=%async_computation.3 | async-start | bytes 4194304 | tf_op jit(solution)/shard_map/psum | solution.py:43
  251.2 143.4 %reduce-scatter.2.cloned.1.call-start = ((), (), s32[]{:S(2)}) async-start(), calls=%async_computation.4 | async-start | bytes 2621440 | tf_op jit(solution)/shard_map/reduce_scatter | solution.py:44
  363.9 103.7 %all-reduce.8.cloned.1.call-start = ((), (), s32[]{:S(2)}) async-start(), calls=%async_computation.5 | async-start | bytes 131072 | tf_op jit(solution)/shard_map/psum | solution.py:48
  394.5 98.5 %copy-start.1 = (f32[1024,128]{0,1:T(8,128)S(1)}, f32[1024,128]{0,1:T(8,128)}, u32[]{:S(2)}) copy-start(f32[1024,128]{0,1:T(8,128)} %reduce-scatter.2.cloned.1.call-done) | copy-start | bytes 1572868
Sparse Core Ops, SparseCore 0:
  9.5 25.5 all-gather.3
  45.4 102.3 all-reduce.3
  164.6 57.5 all-gather.5
  251.3 102.2 all-reduce.5
  364.1 30.4 reduce-scatter.1
  398.4 69.2 all-reduce.7
